TPU v7x, 32 devices: a whole 2x2x4 slice. The times are simulated.
32 devices in a mesh: pipe: 8 (over z, y), tensor: 4 (over x, core).
Axes of the slice: x: 2, y: 2, z: 4, core: 2. Of those that a mesh axis runs over, the one named last changes fastest.
Arguments:
- memory: bfloat16 [2, 512, 4096], P(None, 'pipe', 'tensor'), may hold values from -6 to 6
- states: bfloat16 [8, 2, 256, 4096], P('pipe', None, None, 'tensor'), may hold values from -6 to 6
- norm_gain: float32 [8, 4096], P('pipe'), may hold values from 0.25 to 1.75
- w_query: bfloat16 [8, 4096, 4096], P('pipe', None, 'tensor'), may hold values from -0.09375 to 0.09375
- w_keyvalue: bfloat16 [8, 4096, 2, 4096], P('pipe', None, None, 'tensor'), may hold values from -0.09375 to 0.09375
- w_output: bfloat16 [8, 4096, 4096], P('pipe', 'tensor'), may hold values from -0.125 to 0.125
Outputs:
- updated: bfloat16 [8, 2, 256, 4096], P('pipe', None, None, 'tensor')
All inputs are finite; a program needn't handle non-finite values.
Results may differ from a plain program's by a relative error of at most 0.006.
Values may be sent and summed in bfloat16 or wider, within the bound.
A program may use at most 128 MiB of HBM per device.

v0:
```python
import jax
import jax.numpy as jnp
from jax import lax
from jax.sharding import PartitionSpec as P

HEAD_DIM = 64


def per_device(memory, states, norm_gain, w_query, w_keyvalue, w_output):
    whole_states = lax.all_gather(states[0], "tensor", axis=2, tiled=True)
    xf = whole_states.astype(jnp.float32)
    scale = lax.rsqrt(jnp.mean(xf * xf, axis=-1, keepdims=True) + 1e-06)
    normed = (xf * scale * norm_gain[0]).astype(jnp.bfloat16)
    weight_q = w_query[0]
    local_inner = weight_q.shape[1]
    weight_kv = w_keyvalue[0].reshape(w_keyvalue.shape[1], 2 * local_inner)
    weight_o = w_output[0]
    seqs = normed.shape[0]
    dec_rows = normed.shape[1]
    local_heads = local_inner // HEAD_DIM
    query = jnp.einsum("btd,de->bte", normed, weight_q, preferred_element_type=jnp.float32).astype(
        jnp.bfloat16
    )
    gathered = lax.all_gather(memory, "pipe", axis=1, tiled=True)
    gathered = lax.all_gather(gathered, "tensor", axis=2, tiled=True)
    keyvalue = jnp.einsum(
        "bpd,de->bpe", gathered, weight_kv, preferred_element_type=jnp.float32
    ).astype(jnp.bfloat16)
    enc_rows = keyvalue.shape[1]
    keys = keyvalue[:, :, :local_inner].reshape(seqs, enc_rows, local_heads, HEAD_DIM)
    values = keyvalue[:, :, local_inner:].reshape(seqs, enc_rows, local_heads, HEAD_DIM)
    heads_q = query.reshape(seqs, dec_rows, local_heads, HEAD_DIM)
    scores = jnp.einsum(
        "bqhd,bkhd->bhqk", heads_q, keys, preferred_element_type=jnp.float32
    ) / jnp.sqrt(jnp.float32(HEAD_DIM))
    probs = jax.nn.softmax(scores, axis=-1).astype(jnp.bfloat16)
    context = jnp.einsum(
        "bhqk,bkhd->bqhd", probs, values, preferred_element_type=jnp.float32
    ).astype(jnp.bfloat16)
    context = context.reshape(seqs, dec_rows, local_inner)
    partial_terms = jnp.einsum("bte,ed->btd", context, weight_o, preferred_element_type=jnp.float32)
    branch = lax.psum_scatter(partial_terms, "tensor", scatter_dimension=2, tiled=True)
    result = (states[0].astype(jnp.float32) + branch).astype(jnp.bfloat16)
    return result[None]


def solution(mesh):
    in_specs = (
        P(None, "pipe", "tensor"),
        P("pipe", None, None, "tensor"),
        P("pipe", None),
        P("pipe", None, "tensor"),
        P("pipe", None, None, "tensor"),
        P("pipe", "tensor", None),
    )
    out_specs = P("pipe", None, None, "tensor")
    return jax.shard_map(
        per_device, mesh=mesh, in_specs=in_specs, out_specs=out_specs, check_vma=False
    )
```

profile of v0, /device:TPU:0, one launch (start us, length us, event | category | flops | bytes accessed | tf_op | source)
XLA Modules:
  0.0 294.8 jit_solution(15955444793238928033)
XLA Ops:
  6.5 0.0 all-gather.5.cloned.1.call-start
  6.5 0.7 all-gather.5.cloned.1.call-update
  7.3 0.0 all-gather.9.cloned.1.call-start
  7.3 0.7 all-gather.9.cloned.1.call-update
  8.0 0.0 all-gather.7.cloned.1.call-start
  8.1 53.3 %all-gather.5.cloned.1.call-done = bf16[2,512,1024]{2,1,0:T(8,128)(2,1)} async-done(((bf16[2,64,1024]{2,1,0:T(8,128)(2,1)}), bf16[2,512,1024]{2,1,0:T(8,128)(2,1)}) %all-gather.5.cloned.1.call-update) | async-done | bytes 2097168 | tf_op jit(solution)/shard_map/all_gather | solution.py:24
  61.3 0.0 all-gather.7.cloned.1.call-update
  61.4 0.0 copy-start.2
  61.4 0.0 reduce-scatter.2.cloned.1.call-start
  61.4 28.0 %reshape.30 = bf16[4096,2048,1]{1,0,2:T(8,128)(2,1)} reshape(bf16[1,4096,2,1024]{3,2,1,0:T(2,128)(2,1)} %param.10) | data formatting | bytes 33554432 | tf_op jit(solution)/shard_map/reshape;squeeze | solution.py:16
  89.4 6.5 %all-gather.9.cloned.1.call-done = bf16[1,2,256,4096]{3,2,1,0:T(8,128)(2,1)} async-done(((bf16[1,2,256,1024]{3,2,1,0:T(8,128)(2,1)}), bf16[1,2,256,4096]{3,2,1,0:T(8,128)(2,1)}) %all-gather.9.cloned.1.call-update) | async-done | bytes 4194320 | tf_op jit(solution)/shard_map/all_gather | solution.py:10
  95.9 3.1 %fusion.4 = f32[2,256]{1,0:T(2,128)S(1)} fusion(bf16[1,2,256,4096]{3,2,1,0:T(8,128)(2,1)} %all-gather.9.cloned.1.call-done), kind=kLoop, calls=%fused_computation.7 | loop fusion | flops 6290944 | bytes 4196352 | tf_op jit(solution)/shard_map/reduce_sum | solution.py:12
  99.0 0.0 copy-done.2
  99.0 9.3 %fusion.21 = bf16[2,256,1024]{2,1,0:T(8,128)(2,1)S(1)} fusion(bf16[1,4096,1024]{2,1,0:T(8,128)(2,1)} %param.9, bf16[1,2,256,4096]{3,2,1,0:T(8,128)(2,1)} %all-gather.9.cloned.1.call-done, f32[4096]{0:T(1024)S(1)} %bitcast.43, f32[2,256]{1,0:T(2,128)S(1)} %add_rsqrt_fusion), kind=kOutput, calls=%fused_computation.24 | convolution fusion | flops 4303880192 | bytes 13649920 | tf_op jit(solution)/shard_map/btd,de->bte/dot_general | solution.py:21
  108.4 0.5 copy.12
  108.9 46.9 %all-gather.7.cloned.1.call-done = bf16[2,512,4096]{2,1,0:T(8,128)(2,1)} async-done(((bf16[2,512,1024]{2,1,0:T(8,128)(2,1)}), bf16[2,512,4096]{2,1,0:T(8,128)(2,1)}) %all-gather.7.cloned.1.call-update) | async-done | bytes 8388624 | tf_op jit(solution)/shard_map/all_gather | solution.py:25
  155.8 22.7 %convolution_convert_fusion = bf16[2,512,2048]{2,1,0:T(8,128)(2,1)S(1)} fusion(bf16[2,512,4096]{2,1,0:T(8,128)(2,1)} %all-gather.7.cloned.1.call-done, bf16[4096,2048,1]{1,0,2:T(8,128)(2,1)} %reshape.30), kind=kOutput, calls=%fused_computation.19 | convolution fusion | flops 17181966336 | bytes 29360128 | tf_op jit(solution)/shard_map/bpd,de->bpe/dot_general | solution.py:26
  178.5 1.8 fusion.28
  180.3 3.9 %copy.11 = bf16[2,512,1024]{1,2,0:T(8,128)(2,1)} copy(bf16[2,512,1024]{2,1,0:T(8,128)(2,1)} %get-tuple-element.6) | data formatting | bytes 4194304 | tf_op jit(solution)/shard_map/slice | solution.py:31
  184.2 2.5 copy.13
  186.7 0.0 copy-start.1
  186.7 9.7 %fusion.29 = (f32[2,16,256]{2,1,0:T(8,128)S(1)}, f32[2,16,256,512]{3,2,1,0:T(8,128)}) fusion(bf16[2,256,16,64]{1,3,2,0:T(8,128)(2,1)S(1)} %bitcast.42, bf16[2,512,16,64]{1,3,2,0:T(8,128)(2,1)} %bitcast.40), kind=kOutput, calls=%fused_computation.29 | convolution fusion | flops 549454336 | bytes 19955712 | tf_op jit(solution)/shard_map/sub | solution.py:36
  196.5 0.0 copy-done.1
  196.5 7.3 %fusion.20 = bf16[2,16,64,256]{3,2,1,0:T(8,128)(2,1)S(1)} fusion(bf16[2,512,16,64]{1,3,2,0:T(8,128)(2,1)S(1)} %bitcast.39, f32[2,16,256,512]{3,2,1,0:T(8,128)} %get-tuple-element.8, f32[2,16,256]{2,1,0:T(8,128)S(1)} %get-tuple-element.7), kind=kOutput, calls=%fused_computation.23 | convolution fusion | flops 545783808 | bytes 19955712 | tf_op jit(solution)/shard_map/bhqk,bkhd->bqhd/dot_general | solution.py:37
  203.8 10.2 %fusion.7 = f32[2,256,4096]{2,1,0:T(8,128)} fusion(bf16[2,256,1024]{1,2,0:T(8,128)(2,1)S(1)} %bitcast.41, bf16[1,1024,4096]{2,1,0:T(8,128)(2,1)} %param.11), kind=kOutput, calls=%fused_computation.10 | convolution fusion | flops 4294967296 | bytes 17825792 | tf_op jit(solution)/shard_map/bte,ed->btd/dot_general | solution.py:41
  213.9 0.0 copy-start
  213.9 0.0 reduce-scatter.2.cloned.1.call-update
  214.0 71.4 %reduce-scatter.2.cloned.1.call-done = f32[2,256,1024]{2,1,0:T(8,128)} async-done(((f32[2,256,4096]{2,1,0:T(8,128)}), f32[2,256,1024]{2,1,0:T(8,128)}) %reduce-scatter.2.cloned.1.call-update) | async-done | bytes 2097168 | tf_op jit(solution)/shard_map/reduce_scatter | solution.py:42
  285.4 0.0 copy-done
  285.4 2.9 fusion.26
  (1 shorter events, 0.0 us)
Async XLA Ops:
  6.5 54.8 %all-gather.5.cloned.1.call-start = ((), (), s32[]{:S(2)}) async-start(), calls=%async_computation.1 | async-start | bytes 2359296 | tf_op jit(solution)/shard_map/all_gather | solution.py:24
  7.3 88.7 %all-gather.9.cloned.1.call-start = ((), (), s32[]{:S(2)}) async-start(), calls=%async_computation.4 | async-start | bytes 5242880 | tf_op jit(solution)/shard_map/all_gather | solution.py:10
  8.0 147.8 %all-gather.7.cloned.1.call-start = ((), (), s32[]{:S(2)}) async-start(), calls=%async_computation.2 | async-start | bytes 10485760 | tf_op jit(solution)/shard_map/all_gather | solution.py:25
  61.4 37.7 %copy-start.2 = (f32[1,4096]{1,0:T(1,128)S(1)}, f32[1,4096]{1,0:T(1,128)}, u32[]{:S(2)}) copy-start(f32[1,4096]{1,0:T(1,128)} %param.8) | copy-start | bytes 49156
  61.4 224.0 %reduce-scatter.2.cloned.1.call-start = ((), (), s32[]{:S(2)}) async-start(), calls=%async_computation.3 | async-start | bytes 10485760 | tf_op jit(solution)/shard_map/reduce_scatter | solution.py:42
  186.7 9.8 %copy-start.1 = (bf16[2,512,1024]{1,2,0:T(8,128)(2,1)S(1)}, bf16[2,512,1024]{1,2,0:T(8,128)(2,1)}, u32[]{:S(2)}) copy-start(bf16[2,512,1024]{1,2,0:T(8,128)(2,1)} %copy.11) | copy-start | bytes 6291460
  213.9 71.4 %copy-start = (bf16[1,2,256,1024]{3,2,1,0:T(8,128)(2,1)S(1)}, bf16[1,2,256,1024]{3,2,1,0:T(8,128)(2,1)}, u32[]{:S(2)}) copy-start(bf16[1,2,256,1024]{3,2,1,0:T(8,128)(2,1)} %param.7) | copy-start | bytes 3145732
Sparse Core Ops, SparseCore 0:
  9.5 51.7 all-gather.4
  62.9 32.9 all-gather.8
  97.5 58.2 all-gather.6
  214.1 71.2 reduce-scatter.1
where the time goes:
time: 296 us; the launch traced here: 295 us
  waiting for transfers between devices  180 us (61%)
  matrix products  59.2 us (20%)
  local copies, waits for them, and re-layouts  36.7 us (12%)
  between operations  13.2 us (4%)
  other arithmetic  6 us (2%)
    reduce_scatter x1, waiting for transfers between devices, per_device(): lax.psum_scatter(partial_terms, 'tensor', scatter_dimension=2, tiled=True)  71.4 us
    all_gather x1, waiting for transfers between devices, per_device(): gathered = lax.all_gather(memory, 'pipe', axis=1, tiled=True)  53.3 us
    all_gather x1, waiting for transfers between devices, per_device(): gathered = lax.all_gather(gathered, 'tensor', axis=2, tiled=True)  46.9 us
    another operation x1, local copies, waits for them, and re-layouts, per_device(): weight_kv = w_keyvalue[0].reshape(w_keyvalue.shape[1], 2 * local_inner)  28 us
    dot_general x1, matrix products, per_device(): jnp.einsum('bpd,de->bpe', gathered, weight_kv, preferred_element_type=jnp...  22.7 us
    dot_general x1, matrix products, per_device(): jnp.einsum('bte,ed->btd', context, weight_o, preferred_element_type=jnp.f...  10.2 us
    sub x1, matrix products, per_device(): probs = jax.nn.softmax(scores, axis=-1).astype(jnp.bfloat16)  9.75 us
    dot_general x1, matrix products, per_device(): jnp.einsum('btd,de->bte', normed, weight_q, preferred_element_type=jnp.fl...  9.34 us
  transfers between devices with their start and end apart: 4, of which 4 were waited for; matrix products, arithmetic and copies ran while one was open for 14% of the time, Pallas kernels for 0%

commit v1 on v0

--- a/solution.py
+++ b/solution.py
@@ -22,7 +22,14 @@
         jnp.bfloat16
     )
     gathered = lax.all_gather(memory, "pipe", axis=1, tiled=True)
-    gathered = lax.all_gather(gathered, "tensor", axis=2, tiled=True)
+    ring = [gathered]
+    for hop in range(3):
+        ring.append(lax.ppermute(ring[-1], "tensor", [(dev, (dev + 1) % 4) for dev in range(4)]))
+    gathered = jnp.roll(
+        jnp.concatenate(ring[::-1], axis=2),
+        (lax.axis_index("tensor") + 1) * ring[0].shape[2],
+        axis=2,
+    )
     keyvalue = jnp.einsum(
         "bpd,de->bpe", gathered, weight_kv, preferred_element_type=jnp.float32
     ).astype(jnp.bfloat16)

time: 296 us -> 334 us (1.13)
  local copies, waits for them, and re-layouts: 36.7 us -> 58.4 us
  waiting for transfers between devices: 180 us -> 199 us
    ppermute x0 -> x3, waiting for transfers between devices: none -> 73.7 us  [per_device(): lax.ppermute(ring[-1], 'tensor', [(dev, (dev + 1) % 4) for dev in range(4)])]
    all_gather x1 -> x0, waiting for transfers between devices: 46.9 us -> none  [per_device(): gathered = lax.all_gather(gathered, 'tensor', axis=2, tiled=True)]
    unnamed x6 -> x27, local copies, waits for them, and re-layouts: 0.01 us -> 19.2 us
    all_gather x1, waiting for transfers between devices: 6.53 us -> 0.01 us  [per_device(): whole_states = lax.all_gather(states[0], 'tensor', axis=2, tiled=True)]
  transfers between devices with their start and end apart: 4 -> 6, of which waited for: 4 -> 4; matrix products, arithmetic and copies ran while one was open for 14% -> 13% of each run, Pallas kernels for 0% -> 0%
where the time goes in v1:
time: 334 us; the launch traced here: 333 us
  waiting for transfers between devices  199 us (60%)
  local copies, waits for them, and re-layouts  58.4 us (17%)
  matrix products  57 us (17%)
  between operations  13.2 us (4%)
  other arithmetic  6.01 us (2%)
    ppermute x3, waiting for transfers between devices, per_device(): lax.ppermute(ring[-1], 'tensor', [(dev, (dev + 1) % 4) for dev in range(4)])  73.7 us
    reduce_scatter x1, waiting for transfers between devices, per_device(): lax.psum_scatter(partial_terms, 'tensor', scatter_dimension=2, tiled=True)  70.3 us
    all_gather x1, waiting for transfers between devices, per_device(): gathered = lax.all_gather(memory, 'pipe', axis=1, tiled=True)  53.3 us
    another operation x1, local copies, waits for them, and re-layouts, per_device(): weight_kv = w_keyvalue[0].reshape(w_keyvalue.shape[1], 2 * local_inner)  27.7 us
    dot_general x1, matrix products, per_device(): jnp.einsum('bpd,de->bpe', gathered, weight_kv, preferred_element_type=jnp...  19.6 us
    unnamed x27, local copies, waits for them, and re-layouts  19.2 us
    dot_general x1, matrix products, per_device(): jnp.einsum('bte,ed->btd', context, weight_o, preferred_element_type=jnp.f...  10.2 us
    dot_general x1, matrix products, per_device(): jnp.einsum('btd,de->bte', normed, weight_q, preferred_element_type=jnp.fl...  10.2 us
  transfers between devices with their start and end apart: 6, of which 4 were waited for; matrix products, arithmetic and copies ran while one was open for 13% of the time, Pallas kernels for 0%

profile of v1, /device:TPU:0, one launch (start us, length us, event | category | flops | bytes accessed | tf_op | source)
XLA Modules:
  0.0 333.4 jit_solution(17153845093152811667)
XLA Ops:
  6.5 0.0 all-gather.4.cloned.1.call-start
  6.5 0.7 all-gather.4.cloned.1.call-update
  7.3 0.0 all-gather.6.cloned.1.call-start
  7.3 0.7 all-gather.6.cloned.1.call-update
  8.0 0.0 reduce-scatter.2.cloned.1.call-start
  8.1 53.3 %all-gather.4.cloned.1.call-done = bf16[2,512,1024]{2,1,0:T(8,128)(2,1)} async-done(((bf16[2,64,1024]{2,1,0:T(8,128)(2,1)}), bf16[2,512,1024]{2,1,0:T(8,128)(2,1)}) %all-gather.4.cloned.1.call-update) | async-done | bytes 2097168 | tf_op jit(solution)/shard_map/all_gather | solution.py:24
  61.3 0.0 collective-permute-start
  61.3 48.1 %collective-permute-done = bf16[2,512,1024]{2,1,0:T(8,128)(2,1)S(1)} collective-permute-done((bf16[2,512,1024]{2,1,0:T(8,128)(2,1)}, bf16[2,512,1024]{2,1,0:T(8,128)(2,1)S(1)}, u32[]{:S(2)}, u32[]{:S(2)}) %collective-permute-start) | collective-permute-done | bytes 2097184 | tf_op jit(solution)/shard_map/ppermute | solution.py:27
  109.5 0.0 copy-start.1
  109.5 1.3 copy-done.1
  110.8 0.0 collective-permute-start.1
  110.8 25.6 %collective-permute-done.1 = bf16[2,512,1024]{2,1,0:T(8,128)(2,1)} collective-permute-done((bf16[2,512,1024]{2,1,0:T(8,128)(2,1)S(1)}, bf16[2,512,1024]{2,1,0:T(8,128)(2,1)}, u32[]{:S(2)}, u32[]{:S(2)}) %collective-permute-start.1) | collective-permute-done | bytes 2097184 | tf_op jit(solution)/shard_map/ppermute | solution.py:27
  136.4 0.0 collective-permute-start.2
  136.4 0.0 copy-start.5
  136.4 27.7 %reshape.30 = bf16[4096,2048,1]{1,0,2:T(8,128)(2,1)} reshape(bf16[1,4096,2,1024]{3,2,1,0:T(2,128)(2,1)} %param.10) | data formatting | bytes 33554432 | tf_op jit(solution)/shard_map/reshape;squeeze | solution.py:16
  164.1 3.1 fusion.4
  167.2 0.0 copy-done.5
  167.2 10.2 %fusion.26 = bf16[2,256,1024]{2,1,0:T(8,128)(2,1)} fusion(bf16[1,4096,1024]{2,1,0:T(8,128)(2,1)} %param.9, bf16[1,2,256,4096]{3,2,1,0:T(8,128)(2,1)} %all-gather.6.cloned.1.call-done, f32[4096]{0:T(1024)S(1)} %bitcast.44, f32[2,256]{1,0:T(2,128)S(1)} %add_rsqrt_fusion), kind=kOutput, calls=%fused_computation.26 | convolution fusion | flops 4303880192 | bytes 13649920 | tf_op jit(solution)/shard_map/btd,de->bte/dot_general | solution.py:21
  177.4 1.6 copy.12
  179.0 0.0 copy-start.2
  179.0 0.0 collective-permute-done.2
  179.0 0.0 slice-start
  179.0 3.3 constant_dynamic-update-slice_fusion.7
  182.3 3.1 constant_dynamic-update-slice_fusion.6
  185.4 0.0 copy-done.2
  185.4 1.5 constant_dynamic-update-slice_fusion.5
  186.9 0.0 copy-done
  186.9 1.5 constant_dynamic-update-slice_fusion.4
  188.4 3.2 constant_dynamic-update-slice_fusion.3
  191.6 3.1 constant_dynamic-update-slice_fusion.2
  194.7 1.5 constant_dynamic-update-slice_fusion.1
  196.2 1.5 constant_dynamic-update-slice_fusion
  197.7 0.0 slice-done
  197.7 0.0 slice-done.1
  197.7 0.0 slice-done.2
  197.7 0.6 slice-done.3
  198.4 19.6 %fusion.19 = bf16[2,512,2048]{2,1,0:T(8,128)(2,1)S(1)} fusion(bf16[4096,2048,1]{1,0,2:T(8,128)(2,1)S(1)} %bitcast.39, bf16[2,512,8192]{2,1,0:T(8,128)(2,1)} %constant_dynamic-update-slice_fusion, s32[]{:T(128)S(6)} %select_n.14), kind=kOutput, calls=%fused_computation.21 | convolution fusion | flops 17181966336 | bytes 29360132 | tf_op jit(solution)/shard_map/bpd,de->bpe/dot_general | solution.py:33
  218.0 1.9 fusion.34
  219.8 3.9 %copy.13 = bf16[2,512,1024]{1,2,0:T(8,128)(2,1)} copy(bf16[2,512,1024]{2,1,0:T(8,128)(2,1)} %get-tuple-element.5) | data formatting | bytes 4194304 | tf_op jit(solution)/shard_map/slice | solution.py:37
  223.8 2.6 copy.11
  226.4 9.8 %fusion.35 = (f32[2,16,256]{2,1,0:T(8,128)S(1)}, f32[2,16,256,512]{3,2,1,0:T(8,128)}) fusion(bf16[2,256,16,64]{1,3,2,0:T(8,128)(2,1)S(1)} %bitcast.43, bf16[2,512,16,64]{1,3,2,0:T(8,128)(2,1)} %bitcast.40), kind=kOutput, calls=%fused_computation.40 | convolution fusion | flops 549454336 | bytes 19955712 | tf_op jit(solution)/shard_map/sub | solution.py:43
  236.2 0.0 copy-done.4
  236.2 7.3 %fusion.25 = bf16[2,16,64,256]{3,2,1,0:T(8,128)(2,1)S(1)} fusion(bf16[2,512,16,64]{1,3,2,0:T(8,128)(2,1)S(1)} %bitcast.41, f32[2,16,256,512]{3,2,1,0:T(8,128)} %get-tuple-element.8, f32[2,16,256]{2,1,0:T(8,128)S(1)} %get-tuple-element.7), kind=kOutput, calls=%fused_computation.25 | convolution fusion | flops 545783808 | bytes 19955712 | tf_op jit(solution)/shard_map/bhqk,bkhd->bqhd/dot_general | solution.py:44
  243.4 10.2 %fusion.7 = f32[2,256,4096]{2,1,0:T(8,128)} fusion(bf16[2,256,1024]{1,2,0:T(8,128)(2,1)S(1)} %bitcast.42, bf16[1,1024,4096]{2,1,0:T(8,128)(2,1)} %param.11), kind=kOutput, calls=%fused_computation.10 | convolution fusion | flops 4294967296 | bytes 17825792 | tf_op jit(solution)/shard_map/bte,ed->btd/dot_general | solution.py:48
  253.6 0.0 reduce-scatter.2.cloned.1.call-update
  253.7 70.3 %reduce-scatter.2.cloned.1.call-done = f32[2,256,1024]{2,1,0:T(8,128)} async-done(((f32[2,256,4096]{2,1,0:T(8,128)}), f32[2,256,1024]{2,1,0:T(8,128)}) %reduce-scatter.2.cloned.1.call-update) | async-done | bytes 2097168 | tf_op jit(solution)/shard_map/reduce_scatter | solution.py:49
  323.9 0.0 copy-done.3
  323.9 2.9 fusion.31
  (9 shorter events, 0.0 us)
Async XLA Ops:
  6.5 54.8 %all-gather.4.cloned.1.call-start = ((), (), s32[]{:S(2)}) async-start(), calls=%async_computation.1 | async-start | bytes 2359296 | tf_op jit(solution)/shard_map/all_gather | solution.py:24
  7.3 156.8 %all-gather.6.cloned.1.call-start = ((), (), s32[]{:S(2)}) async-start(), calls=%async_computation.3 | async-start | bytes 5242880 | tf_op jit(solution)/shard_map/all_gather | solution.py:10
  8.0 315.9 %reduce-scatter.2.cloned.1.call-start = ((), (), s32[]{:S(2)}) async-start(), calls=%async_computation.2 | async-start | bytes 10485760 | tf_op jit(solution)/shard_map/reduce_scatter | solution.py:49
  61.3 48.1 %collective-permute-start = (bf16[2,512,1024]{2,1,0:T(8,128)(2,1)}, bf16[2,512,1024]{2,1,0:T(8,128)(2,1)S(1)}, u32[]{:S(2)}, u32[]{:S(2)}) collective-permute-start(bf16[2,512,1024]{2,1,0:T(8,128)(2,1)} %all-gather.4.cloned.1.call-done), channel_id=1, source_target_pairs={{0,1},{1,2},{2,3},{3,0},{4,5},{5,6},{6,7},{7,4},{8,9},{9,10},{10,1... | collective-permute-start | bytes 6291464 | tf_op jit(solution)/shard_map/ppermute | solution.py:27
  109.5 1.3 copy-start.1
  110.8 25.6 %collective-permute-start.1 = (bf16[2,512,1024]{2,1,0:T(8,128)(2,1)S(1)}, bf16[2,512,1024]{2,1,0:T(8,128)(2,1)}, u32[]{:S(2)}, u32[]{:S(2)}) collective-permute-start(bf16[2,512,1024]{2,1,0:T(8,128)(2,1)S(1)} %collective-permute-done), channel_id=1, source_target_pairs={{0,1},{1,2},{2,3},{3,0},{4,5},{5,6},{6,7},{7,4},{8,9},{9,10},{10,1... | collective-permute-start | bytes 6291464 | tf_op jit(solution)/shard_map/ppermute | solution.py:27
  136.4 42.6 %collective-permute-start.2 = (bf16[2,512,1024]{2,1,0:T(8,128)(2,1)}, bf16[2,512,1024]{2,1,0:T(8,128)(2,1)}, u32[]{:S(2)}, u32[]{:S(2)}) collective-permute-start(bf16[2,512,1024]{2,1,0:T(8,128)(2,1)} %collective-permute-done.1), channel_id=1, source_target_pairs={{0,1},{1,2},{2,3},{3,0},{4,5},{5,6},{6,7},{7,4},{8,9},{9,10},{10,1... | collective-permute-start | bytes 6291464 | tf_op jit(solution)/shard_map/ppermute | solution.py:27
  136.4 30.8 %copy-start.5 = (f32[1,4096]{1,0:T(1,128)S(1)}, f32[1,4096]{1,0:T(1,128)}, u32[]{:S(2)}) copy-start(f32[1,4096]{1,0:T(1,128)} %param.8) | copy-start | bytes 49156
  177.4 9.5 %copy-start = (bf16[2,512,1024]{2,1,0:T(8,128)(2,1)S(1)}, bf16[2,512,1024]{2,1,0:T(8,128)(2,1)}, u32[]{:S(2)}) copy-start(bf16[2,512,1024]{2,1,0:T(8,128)(2,1)} %all-gather.4.cloned.1.call-done) | copy-start | bytes 6291460
  179.0 6.4 %copy-start.2 = (bf16[2,512,1024]{2,1,0:T(8,128)(2,1)S(1)}, bf16[2,512,1024]{2,1,0:T(8,128)(2,1)}, u32[]{:S(2)}) copy-start(bf16[2,512,1024]{2,1,0:T(8,128)(2,1)} %copy-done.1) | copy-start | bytes 6291460
  179.0 18.7 %slice-start = ((s8[16777216]{0:T(1024)(128)(4,1)}), s8[4194304]{0:T(1024)(128)(4,1)S(1)}, s32[]{:S(2)}) async-start(s8[16777216]{0:T(1024)(128)(4,1)} %bitcast.38), calls=%async_computation.4 | async-start | bytes 8388608
  185.4 12.3 %slice-start.1 = ((s8[16777216]{0:T(1024)(128)(4,1)}), s8[4194304]{0:T(1024)(128)(4,1)S(1)}, s32[]{:S(2)}) async-start(s8[16777216]{0:T(1024)(128)(4,1)} %bitcast.38), calls=%async_computation.5 | async-start | bytes 8388608
  188.3 9.4 %slice-start.2 = ((s8[16777216]{0:T(1024)(128)(4,1)}), s8[4194304]{0:T(1024)(128)(4,1)S(1)}, s32[]{:S(2)}) async-start(s8[16777216]{0:T(1024)(128)(4,1)} %bitcast.38), calls=%async_computation.6 | async-start | bytes 8388608
  194.6 3.7 %slice-start.3 = ((s8[16777216]{0:T(1024)(128)(4,1)}), s8[4194304]{0:T(1024)(128)(4,1)S(1)}, s32[]{:S(2)}) async-start(s8[16777216]{0:T(1024)(128)(4,1)} %bitcast.38), calls=%async_computation.7 | async-start | bytes 8388608
  226.4 9.8 %copy-start.4 = (bf16[2,512,1024]{1,2,0:T(8,128)(2,1)S(1)}, bf16[2,512,1024]{1,2,0:T(8,128)(2,1)}, u32[]{:S(2)}) copy-start(bf16[2,512,1024]{1,2,0:T(8,128)(2,1)} %copy.11) | copy-start | bytes 6291460
  253.6 70.3 %copy-start.3 = (bf16[1,2,256,1024]{3,2,1,0:T(8,128)(2,1)S(1)}, bf16[1,2,256,1024]{3,2,1,0:T(8,128)(2,1)}, u32[]{:S(2)}) copy-start(bf16[1,2,256,1024]{3,2,1,0:T(8,128)(2,1)} %param.7) | copy-start | bytes 3145732
Sparse Core Ops, SparseCore 0:
  9.5 51.7 all-gather.3
  62.9 44.3 all-gather.5
  253.8 70.1 reduce-scatter.1
